TPU v7x, 32 devices: a whole 2x2x4 slice. The times are simulated.
32 devices in a mesh: slab: 8 (over z, y), plane: 4 (over x, core).
Axes of the slice: x: 2, y: 2, z: 4, core: 2. Of those that a mesh axis runs over, the one named last changes fastest.
Arguments:
- tissue_v: float32 [32, 64, 128], P('slab', 'plane'), may hold values from -4 to 4
- tissue_gates: float32 [40, 32, 64, 128], P(None, 'slab', 'plane'), may hold values from 0 to 1
- tissue_diff: float32 [32, 64, 128], P('slab', 'plane'), may hold values from 0.2 to 1
- fibre_v: float32 [128, 2048], P('slab', 'plane'), may hold values from -4 to 4
- fibre_gates: float32 [40, 128, 2048], P(None, 'slab', 'plane'), may hold values from 0 to 1
- fibre_diff: float32 [128, 2048], P('slab', 'plane'), may hold values from 0.2 to 1
- gate_half: float32 [40], replicated, may hold values from -3 to 3
- gate_rate: float32 [40], replicated, may hold values from 0.5 to 20
- gate_cond: float32 [40], replicated, may hold values from 0.01 to 0.15
- gate_rev: float32 [40], replicated, may hold values from -2 to 2
- junc_cond: float32 [8], replicated, may hold values from 0.25 to 2
- junc_fibre: int32 [131072], P(('slab', 'plane')), may hold values from 0 to 15
- junc_fcell: int32 [131072], P(('slab', 'plane')), may hold values from 0 to 511
- junc_owner: int32 [131072, 1], P(('slab', 'plane')), may hold values from 0 to 31; in each aligned block of 4096 rows (0 to 4095, 4096 to 8191, ...) at most 256 rows name the same one
- junc_tcell: int32 [131072], P(('slab', 'plane')), may hold values from 0 to 8191
- junc_class: int32 [131072], P(('slab', 'plane')), may hold values from 0 to 7
Outputs:
- tissue_out: float32 [32, 64, 128], P('slab', 'plane')
- fibre_out: float32 [128, 2048], P('slab', 'plane')
Inputs may be any that keep to these rules, and one draw needn't show every extreme that they name: `junc_owner`: among the junctions held by one device, no tissue block is named by more than 256 of them, and some block is named by exactly 256. `junc_fibre`: A fibre of the slab group of the device that holds the junction. `junc_fcell`: A cell of the holding device's share of that fibre. `junc_tcell`: numbered over the owner's block in the order z, y, x with x fastest.
All inputs are finite; a program needn't handle non-finite values.
Results may differ from a plain program's by a relative error of at most 0.00005.
Values sent between devices are 32-bit elements; how exact they have to be, the bound alone decides.
A program may use at most 64 MiB of HBM per device.

v0:
```python
import jax
import jax.numpy as jnp
from jax import lax
from jax.sharding import PartitionSpec as P

STEPS = 14
time_step = 0.1
gate_slope = 2.0


def shift_pair(up, down, axis):
    count = lax.axis_size(axis)
    forward = [(i, i + 1) for i in range(count - 1)]
    backward = [(target, source) for source, target in forward]
    return (lax.ppermute(up, axis, forward), lax.ppermute(down, axis, backward))


def membrane(voltage, gates, gate_half, gate_rate, gate_cond, gate_rev):
    gate_shape = (gates.shape[0],) + (1,) * (gates.ndim - 1)
    gate_signs = (
        jnp.where(jnp.arange(gates.shape[0], dtype=jnp.int32) % 2 == 0, 1.0, -1.0)
        .astype(jnp.float32)
        .reshape(gate_shape)
    )
    shifted = voltage[None] - gate_half.reshape(gate_shape)
    steady = jax.nn.sigmoid(gate_signs * gate_slope * shifted)
    decay_factor = jnp.exp(
        -time_step * gate_rate.reshape(gate_shape) * (1.0 + jax.nn.sigmoid(shifted))
    )
    renewed = steady + (gates - steady) * decay_factor
    driving = gate_cond.reshape(gate_shape) * (voltage[None] - gate_rev.reshape(gate_shape))
    return (renewed, jnp.sum(driving * renewed, axis=0))


def line_count(length, offset, total):
    places = offset + jnp.arange(length, dtype=jnp.int32)
    return (places > 0).astype(jnp.float32) + (places < total - 1).astype(jnp.float32)


def class_gain(classes, junc_cond):
    return jnp.sum(
        jnp.where(
            classes[:, None] == jnp.arange(junc_cond.shape[0], dtype=jnp.int32)[None, :],
            junc_cond[None, :],
            jnp.zeros((), jnp.float32),
        ),
        axis=1,
    )


def make_onehot(indices, count):
    return (indices[:, None] == jnp.arange(count, dtype=jnp.int32)[None, :]).astype(jnp.float32)


def split_two(values):
    high = lax.reduce_precision(values, 8, 7)
    low = lax.reduce_precision(values - high, 8, 7)
    return (high, low)


def pick_split(rows, cols, table):
    depth, width = table.shape
    high, low = split_two(table)
    stacked = jnp.concatenate([high, low], axis=0).astype(jnp.bfloat16)
    onehot = rows[:, None] == (jnp.arange(2 * depth, dtype=jnp.int32) % depth)[None, :]
    rows_read = jnp.dot(onehot.astype(jnp.bfloat16), stacked, preferred_element_type=jnp.float32)
    chosen = cols[:, None] == jnp.arange(width, dtype=jnp.int32)[None, :]
    return jnp.sum(jnp.where(chosen, rows_read, 0.0), axis=1)


def place_split(rows, cols, values, depth, width):
    high, low = split_two(values)
    lanes = jnp.arange(2 * width, dtype=jnp.int32)
    both = jnp.where((lanes < width)[None, :], high[:, None], low[:, None])
    weighted = jnp.where(cols[:, None] == (lanes % width)[None, :], both, 0.0)
    onehot = (rows[:, None] == jnp.arange(depth, dtype=jnp.int32)[None, :]).astype(jnp.bfloat16)
    halves = lax.dot_general(
        onehot,
        weighted.astype(jnp.bfloat16),
        (((0,), (0,)), ((), ())),
        preferred_element_type=jnp.float32,
    )
    return halves[:, :width] + halves[:, width:]


def running_rank(owner_onehot):
    total, kinds = owner_onehot.shape
    tall = 128
    blocks = owner_onehot.astype(jnp.bfloat16).reshape(total // tall, tall, kinds)
    lower = jnp.tril(jnp.ones((tall, tall), jnp.bfloat16))
    within = jnp.einsum("ij,bjo->bio", lower, blocks, preferred_element_type=jnp.float32)
    sums = within[:, -1, :]
    count = total // tall
    before = jnp.tril(jnp.ones((count, count), jnp.float32), -1)
    ahead = jnp.dot(before, sums, precision=lax.Precision.HIGHEST)
    ranks = jnp.sum((within + ahead[:, None, :]).reshape(total, kinds) * owner_onehot, axis=1)
    return jnp.round(ranks).astype(jnp.int32) - 1


def place_values(row_onehot, col_onehot, values):
    weighted = col_onehot * values[:, None]
    return lax.dot_general(
        row_onehot,
        weighted,
        (((0,), (0,)), ((), ())),
        precision=lax.Precision.HIGHEST,
        preferred_element_type=jnp.float32,
    )


def trade_both(paired):
    return lax.all_to_all(paired, ("slab", "plane"), split_axis=1, concat_axis=1, tiled=True)


def body(
    tissue_v,
    tissue_gates,
    tissue_diff,
    fibre_v,
    fibre_gates,
    fibre_diff,
    gate_half,
    gate_rate,
    gate_cond,
    gate_rev,
    junc_cond,
    junc_fibre,
    junc_fcell,
    junc_owner,
    junc_tcell,
    junc_class,
):
    slab_count = lax.axis_size("slab")
    plane_count = lax.axis_size("plane")
    devices = slab_count * plane_count
    layers_dev, rows_dev, cols_dev = tissue_v.shape
    fibre_rows, fibre_cols = fibre_v.shape
    junctions = junc_fibre.shape[0]
    capacity = 2 * junctions // devices
    tissue_count = (
        line_count(layers_dev, lax.axis_index("slab") * layers_dev, layers_dev * slab_count)[
            :, None, None
        ]
        + line_count(rows_dev, lax.axis_index("plane") * rows_dev, rows_dev * plane_count)[
            None, :, None
        ]
        + line_count(cols_dev, 0, cols_dev)[None, None, :]
    )
    fibre_count = line_count(
        fibre_cols, lax.axis_index("plane") * fibre_cols, fibre_cols * plane_count
    )[None, :]
    fibre_cells = fibre_rows * fibre_cols
    fibre_width = 128
    fibre_grid_rows = fibre_cells // fibre_width
    tissue_grid_rows = layers_dev * rows_dev
    owners = junc_owner[:, 0]
    owner_onehot = make_onehot(owners, devices)
    rank_onehot = make_onehot(running_rank(owner_onehot), capacity)
    kinds = junc_cond.shape[0] + 1
    code = (junc_tcell * kinds + junc_class + 1).astype(jnp.float32)
    code_table = jnp.round(place_values(owner_onehot, rank_onehot, code)).astype(jnp.int32)
    fibre_index = (junc_fibre * fibre_cols + junc_fcell).astype(jnp.float32)
    fibre_table = jnp.round(place_values(owner_onehot, rank_onehot, fibre_index))
    own_cells = fibre_table.astype(jnp.int32).reshape(-1)
    sent_tables = jnp.stack([code_table // kinds, code_table % kinds - 1])
    got_tables = lax.all_to_all(
        sent_tables, ("slab", "plane"), split_axis=1, concat_axis=1, tiled=True
    )
    remote_cells = got_tables[0].reshape(-1)
    remote_gain = class_gain(got_tables[1].reshape(-1), junc_cond)
    own_gain = class_gain(sent_tables[1].reshape(-1), junc_cond)
    fibre_at_row, fibre_at_col = (own_cells // fibre_width, own_cells % fibre_width)
    cell_row, cell_col = (remote_cells // cols_dev, remote_cells % cols_dev)

    def advance(step_index, carry):
        tissue_now, tissue_state, fibre_now, fibre_state = carry
        fibre_grid = fibre_now.reshape(fibre_grid_rows, fibre_width)
        tissue_grid = tissue_now.reshape(tissue_grid_rows, cols_dev)
        end_pad = (0, cols_dev - fibre_rows)
        up = jnp.concatenate([tissue_now[:, -1], jnp.pad(fibre_now[:, -1], end_pad)[None]])
        down = jnp.concatenate([tissue_now[:, 0], jnp.pad(fibre_now[:, 0], end_pad)[None]])
        y_low, y_high = shift_pair(up, down, "plane")
        z_low, z_high = shift_pair(tissue_now[-1:], tissue_now[:1], "slab")
        fibre_at_slot = pick_split(fibre_at_row, fibre_at_col, fibre_grid)
        tissue_at_slot = pick_split(cell_row, cell_col, tissue_grid)
        paired = jnp.stack([fibre_at_slot, tissue_at_slot]).reshape(2, devices, capacity)
        traded = trade_both(paired).reshape(2, -1)
        current = remote_gain * (traded[0] - tissue_at_slot)
        fibre_current = own_gain * (fibre_at_slot - traded[1])
        tissue_source = place_split(
            cell_row, cell_col, current, tissue_grid_rows, cols_dev
        ).reshape(tissue_now.shape)
        fibre_source = place_split(
            fibre_at_row, fibre_at_col, fibre_current, fibre_grid_rows, fibre_width
        ).reshape(fibre_now.shape)
        sides = jnp.pad(tissue_now, ((0, 0), (0, 0), (1, 1)))
        neighbours = (
            jnp.concatenate([tissue_now[1:], z_high], axis=0)
            + jnp.concatenate([z_low, tissue_now[:-1]], axis=0)
            + jnp.concatenate([tissue_now[:, 1:], y_high[:-1, None]], axis=1)
            + jnp.concatenate([y_low[:-1, None], tissue_now[:, :-1]], axis=1)
            + sides[:, :, 2:]
            + sides[:, :, :-2]
        )
        tissue_lap = neighbours - tissue_count * tissue_now
        fibre_lap = (
            jnp.concatenate([fibre_now[:, 1:], y_high[-1, :fibre_rows, None]], axis=1)
            + jnp.concatenate([y_low[-1, :fibre_rows, None], fibre_now[:, :-1]], axis=1)
            - fibre_count * fibre_now
        )
        tissue_state, tissue_ionic = membrane(
            tissue_now, tissue_state, gate_half, gate_rate, gate_cond, gate_rev
        )
        fibre_state, fibre_ionic = membrane(
            fibre_now, fibre_state, gate_half, gate_rate, gate_cond, gate_rev
        )
        tissue_next = tissue_now + time_step * (
            tissue_diff * tissue_lap - tissue_ionic + tissue_source
        )
        fibre_next = fibre_now + time_step * (fibre_diff * fibre_lap - fibre_ionic - fibre_source)
        return (tissue_next, tissue_state, fibre_next, fibre_state)

    final = lax.fori_loop(0, STEPS, advance, (tissue_v, tissue_gates, fibre_v, fibre_gates))
    return (final[0], final[2])


def solution(mesh):
    in_specs = (
        P("slab", "plane", None),
        P(None, "slab", "plane", None),
        P("slab", "plane", None),
        P("slab", "plane"),
        P(None, "slab", "plane"),
        P("slab", "plane"),
        P(),
        P(),
        P(),
        P(),
        P(),
        P(("slab", "plane")),
        P(("slab", "plane")),
        P(("slab", "plane"), None),
        P(("slab", "plane")),
        P(("slab", "plane")),
    )
    out_specs = (P("slab", "plane", None), P("slab", "plane"))
    return jax.shard_map(body, mesh=mesh, in_specs=in_specs, out_specs=out_specs, check_vma=False)
```

profile of v0, /device:TPU:0, one launch (start us, length us, event | category | flops | bytes accessed | tf_op | source)
XLA Modules:
  0.0 494.1 jit_solution(6374147802733579538)
XLA Ops:
  5.3 7.3 %all-to-all-start.1 = ((s32[2,32,256]{2,0,1:T(2,128)}), s32[2,32,256]{2,0,1:T(2,128)S(1)}, u32[]{:S(2)}, u32[]{:S(2)}) async-start(s32[2,32,256]{2,0,1:T(2,128)} %copy.60), calls=%async_computation.1 | async-start | bytes 131072 | tf_op jit(solution)/shard_map/all_to_all | solution.py:166
  14.7 5.3 %all-to-all-done.1 = s32[2,32,256]{2,0,1:T(2,128)S(1)} async-done(((s32[2,32,256]{2,0,1:T(2,128)}), s32[2,32,256]{2,0,1:T(2,128)S(1)}, u32[]{:S(2)}, u32[]{:S(2)}) %all-to-all-start.1) | async-done | bytes 65568 | tf_op jit(solution)/shard_map/all_to_all | solution.py:166
  20.5 472.9 %while.20 = (s32[]{:T(128)}, f32[4,16,128]{2,1,0:T(8,128)S(1)}, f32[40,4,16,128]{3,2,1,0:T(8,128)S(1)}, f32[16,512]{1,0:T(8,128)S(1)}, f32[40,16,512]{2,1,0:T(8,...) while((s32[]{:T(128)}, f32[4,16,128]{2,1,0:T(8,128)S(1)}, ...), condition=%wide.region_8.9_spmd.clone, body=%wide.region_3.8_spmd.clone.sunk | while | flops 1107442944 | bytes 8335497 | solution.py:223
  34.9 4.9 all-to-all-start
  42.5 4.6 all-to-all-done
  68.6 4.9 all-to-all-start
  76.3 4.6 all-to-all-done
  102.4 4.9 all-to-all-start
  110.0 4.6 all-to-all-done
  136.2 4.9 all-to-all-start
  143.8 4.6 all-to-all-done
  169.9 4.9 all-to-all-start
  177.6 4.6 all-to-all-done
  203.7 4.9 all-to-all-start
  211.3 4.6 all-to-all-done
  237.5 4.9 all-to-all-start
  245.1 4.6 all-to-all-done
  271.2 4.9 all-to-all-start
  305.0 4.9 all-to-all-start
  338.8 4.9 all-to-all-start
  372.5 4.9 all-to-all-start
  406.3 4.9 all-to-all-start
  440.1 4.9 all-to-all-start
  473.8 4.9 all-to-all-start
  (834 shorter events, 374.6 us)
Async XLA Ops:
  20.7 33.6 %collective-permute-start = (f32[1,16,128]{2,1,0:T(8,128)S(1)}, f32[1,16,128]{2,1,0:T(8,128)S(1)}, u32[]{:S(2)}, u32[]{:S(2)}) collective-permute-start(f32[1,16,128]{2,1,0:T(8,128)S(1)} %get-tuple-element.600), channel_id=1, source_target_pairs={{4,0},{8,4},{12,8},{16,12},{20,16},{24,20},{28,24},{5,1},{9,5},{13... | collective-permute-start | bytes 24584 | tf_op jit(solution)/shard_map/while/body/eval_jaxpr/ppermute | solution.py:15
  22.0 32.3 %collective-permute-start.1 = (f32[1,16,128]{2,1,0:T(8,128)S(1)}, f32[1,16,128]{2,1,0:T(8,128)S(1)}, u32[]{:S(2)}, u32[]{:S(2)}) collective-permute-start(f32[1,16,128]{2,1,0:T(8,128)S(1)} %get-tuple-element.603), channel_id=1, source_target_pairs={{0,4},{4,8},{8,12},{12,16},{16,20},{20,24},{24,28},{1,5},{5,9},{9,... | collective-permute-start | bytes 24584 | tf_op jit(solution)/shard_map/while/body/eval_jaxpr/ppermute | solution.py:15
  54.5 33.6 %collective-permute-start = (f32[1,16,128]{2,1,0:T(8,128)S(1)}, f32[1,16,128]{2,1,0:T(8,128)S(1)}, u32[]{:S(2)}, u32[]{:S(2)}) collective-permute-start(f32[1,16,128]{2,1,0:T(8,128)S(1)} %get-tuple-element.600), channel_id=1, source_target_pairs={{4,0},{8,4},{12,8},{16,12},{20,16},{24,20},{28,24},{5,1},{9,5},{13... | collective-permute-start | bytes 24584 | tf_op jit(solution)/shard_map/while/body/eval_jaxpr/ppermute | solution.py:15
  55.8 32.3 %collective-permute-start.1 = (f32[1,16,128]{2,1,0:T(8,128)S(1)}, f32[1,16,128]{2,1,0:T(8,128)S(1)}, u32[]{:S(2)}, u32[]{:S(2)}) collective-permute-start(f32[1,16,128]{2,1,0:T(8,128)S(1)} %get-tuple-element.603), channel_id=1, source_target_pairs={{0,4},{4,8},{8,12},{12,16},{16,20},{20,24},{24,28},{1,5},{5,9},{9,... | collective-permute-start | bytes 24584 | tf_op jit(solution)/shard_map/while/body/eval_jaxpr/ppermute | solution.py:15
  88.2 33.6 %collective-permute-start = (f32[1,16,128]{2,1,0:T(8,128)S(1)}, f32[1,16,128]{2,1,0:T(8,128)S(1)}, u32[]{:S(2)}, u32[]{:S(2)}) collective-permute-start(f32[1,16,128]{2,1,0:T(8,128)S(1)} %get-tuple-element.600), channel_id=1, source_target_pairs={{4,0},{8,4},{12,8},{16,12},{20,16},{24,20},{28,24},{5,1},{9,5},{13... | collective-permute-start | bytes 24584 | tf_op jit(solution)/shard_map/while/body/eval_jaxpr/ppermute | solution.py:15
  89.5 32.3 %collective-permute-start.1 = (f32[1,16,128]{2,1,0:T(8,128)S(1)}, f32[1,16,128]{2,1,0:T(8,128)S(1)}, u32[]{:S(2)}, u32[]{:S(2)}) collective-permute-start(f32[1,16,128]{2,1,0:T(8,128)S(1)} %get-tuple-element.603), channel_id=1, source_target_pairs={{0,4},{4,8},{8,12},{12,16},{16,20},{20,24},{24,28},{1,5},{5,9},{9,... | collective-permute-start | bytes 24584 | tf_op jit(solution)/shard_map/while/body/eval_jaxpr/ppermute | solution.py:15
  122.0 33.6 %collective-permute-start = (f32[1,16,128]{2,1,0:T(8,128)S(1)}, f32[1,16,128]{2,1,0:T(8,128)S(1)}, u32[]{:S(2)}, u32[]{:S(2)}) collective-permute-start(f32[1,16,128]{2,1,0:T(8,128)S(1)} %get-tuple-element.600), channel_id=1, source_target_pairs={{4,0},{8,4},{12,8},{16,12},{20,16},{24,20},{28,24},{5,1},{9,5},{13... | collective-permute-start | bytes 24584 | tf_op jit(solution)/shard_map/while/body/eval_jaxpr/ppermute | solution.py:15
  123.3 32.3 %collective-permute-start.1 = (f32[1,16,128]{2,1,0:T(8,128)S(1)}, f32[1,16,128]{2,1,0:T(8,128)S(1)}, u32[]{:S(2)}, u32[]{:S(2)}) collective-permute-start(f32[1,16,128]{2,1,0:T(8,128)S(1)} %get-tuple-element.603), channel_id=1, source_target_pairs={{0,4},{4,8},{8,12},{12,16},{16,20},{20,24},{24,28},{1,5},{5,9},{9,... | collective-permute-start | bytes 24584 | tf_op jit(solution)/shard_map/while/body/eval_jaxpr/ppermute | solution.py:15
  155.8 33.6 %collective-permute-start = (f32[1,16,128]{2,1,0:T(8,128)S(1)}, f32[1,16,128]{2,1,0:T(8,128)S(1)}, u32[]{:S(2)}, u32[]{:S(2)}) collective-permute-start(f32[1,16,128]{2,1,0:T(8,128)S(1)} %get-tuple-element.600), channel_id=1, source_target_pairs={{4,0},{8,4},{12,8},{16,12},{20,16},{24,20},{28,24},{5,1},{9,5},{13... | collective-permute-start | bytes 24584 | tf_op jit(solution)/shard_map/while/body/eval_jaxpr/ppermute | solution.py:15
  157.1 32.3 %collective-permute-start.1 = (f32[1,16,128]{2,1,0:T(8,128)S(1)}, f32[1,16,128]{2,1,0:T(8,128)S(1)}, u32[]{:S(2)}, u32[]{:S(2)}) collective-permute-start(f32[1,16,128]{2,1,0:T(8,128)S(1)} %get-tuple-element.603), channel_id=1, source_target_pairs={{0,4},{4,8},{8,12},{12,16},{16,20},{20,24},{24,28},{1,5},{5,9},{9,... | collective-permute-start | bytes 24584 | tf_op jit(solution)/shard_map/while/body/eval_jaxpr/ppermute | solution.py:15
  189.5 33.6 %collective-permute-start = (f32[1,16,128]{2,1,0:T(8,128)S(1)}, f32[1,16,128]{2,1,0:T(8,128)S(1)}, u32[]{:S(2)}, u32[]{:S(2)}) collective-permute-start(f32[1,16,128]{2,1,0:T(8,128)S(1)} %get-tuple-element.600), channel_id=1, source_target_pairs={{4,0},{8,4},{12,8},{16,12},{20,16},{24,20},{28,24},{5,1},{9,5},{13... | collective-permute-start | bytes 24584 | tf_op jit(solution)/shard_map/while/body/eval_jaxpr/ppermute | solution.py:15
  223.3 33.6 %collective-permute-start = (f32[1,16,128]{2,1,0:T(8,128)S(1)}, f32[1,16,128]{2,1,0:T(8,128)S(1)}, u32[]{:S(2)}, u32[]{:S(2)}) collective-permute-start(f32[1,16,128]{2,1,0:T(8,128)S(1)} %get-tuple-element.600), channel_id=1, source_target_pairs={{4,0},{8,4},{12,8},{16,12},{20,16},{24,20},{28,24},{5,1},{9,5},{13... | collective-permute-start | bytes 24584 | tf_op jit(solution)/shard_map/while/body/eval_jaxpr/ppermute | solution.py:15
  257.1 33.6 %collective-permute-start = (f32[1,16,128]{2,1,0:T(8,128)S(1)}, f32[1,16,128]{2,1,0:T(8,128)S(1)}, u32[]{:S(2)}, u32[]{:S(2)}) collective-permute-start(f32[1,16,128]{2,1,0:T(8,128)S(1)} %get-tuple-element.600), channel_id=1, source_target_pairs={{4,0},{8,4},{12,8},{16,12},{20,16},{24,20},{28,24},{5,1},{9,5},{13... | collective-permute-start | bytes 24584 | tf_op jit(solution)/shard_map/while/body/eval_jaxpr/ppermute | solution.py:15
  290.8 33.6 %collective-permute-start = (f32[1,16,128]{2,1,0:T(8,128)S(1)}, f32[1,16,128]{2,1,0:T(8,128)S(1)}, u32[]{:S(2)}, u32[]{:S(2)}) collective-permute-start(f32[1,16,128]{2,1,0:T(8,128)S(1)} %get-tuple-element.600), channel_id=1, source_target_pairs={{4,0},{8,4},{12,8},{16,12},{20,16},{24,20},{28,24},{5,1},{9,5},{13... | collective-permute-start | bytes 24584 | tf_op jit(solution)/shard_map/while/body/eval_jaxpr/ppermute | solution.py:15
  324.6 33.6 %collective-permute-start = (f32[1,16,128]{2,1,0:T(8,128)S(1)}, f32[1,16,128]{2,1,0:T(8,128)S(1)}, u32[]{:S(2)}, u32[]{:S(2)}) collective-permute-start(f32[1,16,128]{2,1,0:T(8,128)S(1)} %get-tuple-element.600), channel_id=1, source_target_pairs={{4,0},{8,4},{12,8},{16,12},{20,16},{24,20},{28,24},{5,1},{9,5},{13... | collective-permute-start | bytes 24584 | tf_op jit(solution)/shard_map/while/body/eval_jaxpr/ppermute | solution.py:15
  325.9 32.3 %collective-permute-start.1 = (f32[1,16,128]{2,1,0:T(8,128)S(1)}, f32[1,16,128]{2,1,0:T(8,128)S(1)}, u32[]{:S(2)}, u32[]{:S(2)}) collective-permute-start(f32[1,16,128]{2,1,0:T(8,128)S(1)} %get-tuple-element.603), channel_id=1, source_target_pairs={{0,4},{4,8},{8,12},{12,16},{16,20},{20,24},{24,28},{1,5},{5,9},{9,... | collective-permute-start | bytes 24584 | tf_op jit(solution)/shard_map/while/body/eval_jaxpr/ppermute | solution.py:15
  358.4 33.6 %collective-permute-start = (f32[1,16,128]{2,1,0:T(8,128)S(1)}, f32[1,16,128]{2,1,0:T(8,128)S(1)}, u32[]{:S(2)}, u32[]{:S(2)}) collective-permute-start(f32[1,16,128]{2,1,0:T(8,128)S(1)} %get-tuple-element.600), channel_id=1, source_target_pairs={{4,0},{8,4},{12,8},{16,12},{20,16},{24,20},{28,24},{5,1},{9,5},{13... | collective-permute-start | bytes 24584 | tf_op jit(solution)/shard_map/while/body/eval_jaxpr/ppermute | solution.py:15
  359.7 32.3 %collective-permute-start.1 = (f32[1,16,128]{2,1,0:T(8,128)S(1)}, f32[1,16,128]{2,1,0:T(8,128)S(1)}, u32[]{:S(2)}, u32[]{:S(2)}) collective-permute-start(f32[1,16,128]{2,1,0:T(8,128)S(1)} %get-tuple-element.603), channel_id=1, source_target_pairs={{0,4},{4,8},{8,12},{12,16},{16,20},{20,24},{24,28},{1,5},{5,9},{9,... | collective-permute-start | bytes 24584 | tf_op jit(solution)/shard_map/while/body/eval_jaxpr/ppermute | solution.py:15
  392.1 33.6 %collective-permute-start = (f32[1,16,128]{2,1,0:T(8,128)S(1)}, f32[1,16,128]{2,1,0:T(8,128)S(1)}, u32[]{:S(2)}, u32[]{:S(2)}) collective-permute-start(f32[1,16,128]{2,1,0:T(8,128)S(1)} %get-tuple-element.600), channel_id=1, source_target_pairs={{4,0},{8,4},{12,8},{16,12},{20,16},{24,20},{28,24},{5,1},{9,5},{13... | collective-permute-start | bytes 24584 | tf_op jit(solution)/shard_map/while/body/eval_jaxpr/ppermute | solution.py:15
  393.4 32.3 %collective-permute-start.1 = (f32[1,16,128]{2,1,0:T(8,128)S(1)}, f32[1,16,128]{2,1,0:T(8,128)S(1)}, u32[]{:S(2)}, u32[]{:S(2)}) collective-permute-start(f32[1,16,128]{2,1,0:T(8,128)S(1)} %get-tuple-element.603), channel_id=1, source_target_pairs={{0,4},{4,8},{8,12},{12,16},{16,20},{20,24},{24,28},{1,5},{5,9},{9,... | collective-permute-start | bytes 24584 | tf_op jit(solution)/shard_map/while/body/eval_jaxpr/ppermute | solution.py:15
  425.9 33.6 %collective-permute-start = (f32[1,16,128]{2,1,0:T(8,128)S(1)}, f32[1,16,128]{2,1,0:T(8,128)S(1)}, u32[]{:S(2)}, u32[]{:S(2)}) collective-permute-start(f32[1,16,128]{2,1,0:T(8,128)S(1)} %get-tuple-element.600), channel_id=1, source_target_pairs={{4,0},{8,4},{12,8},{16,12},{20,16},{24,20},{28,24},{5,1},{9,5},{13... | collective-permute-start | bytes 24584 | tf_op jit(solution)/shard_map/while/body/eval_jaxpr/ppermute | solution.py:15
  427.2 32.3 %collective-permute-start.1 = (f32[1,16,128]{2,1,0:T(8,128)S(1)}, f32[1,16,128]{2,1,0:T(8,128)S(1)}, u32[]{:S(2)}, u32[]{:S(2)}) collective-permute-start(f32[1,16,128]{2,1,0:T(8,128)S(1)} %get-tuple-element.603), channel_id=1, source_target_pairs={{0,4},{4,8},{8,12},{12,16},{16,20},{20,24},{24,28},{1,5},{5,9},{9,... | collective-permute-start | bytes 24584 | tf_op jit(solution)/shard_map/while/body/eval_jaxpr/ppermute | solution.py:15
  459.7 33.6 %collective-permute-start = (f32[1,16,128]{2,1,0:T(8,128)S(1)}, f32[1,16,128]{2,1,0:T(8,128)S(1)}, u32[]{:S(2)}, u32[]{:S(2)}) collective-permute-start(f32[1,16,128]{2,1,0:T(8,128)S(1)} %get-tuple-element.600), channel_id=1, source_target_pairs={{4,0},{8,4},{12,8},{16,12},{20,16},{24,20},{28,24},{5,1},{9,5},{13... | collective-permute-start | bytes 24584 | tf_op jit(solution)/shard_map/while/body/eval_jaxpr/ppermute | solution.py:15
  461.0 32.3 %collective-permute-start.1 = (f32[1,16,128]{2,1,0:T(8,128)S(1)}, f32[1,16,128]{2,1,0:T(8,128)S(1)}, u32[]{:S(2)}, u32[]{:S(2)}) collective-permute-start(f32[1,16,128]{2,1,0:T(8,128)S(1)} %get-tuple-element.603), channel_id=1, source_target_pairs={{0,4},{4,8},{8,12},{12,16},{16,20},{20,24},{24,28},{1,5},{5,9},{9,... | collective-permute-start | bytes 24584 | tf_op jit(solution)/shard_map/while/body/eval_jaxpr/ppermute | solution.py:15
  (121 other events, 1160.1 us)
where the time goes:
time: 496 us; the launch traced here: 494 us
  starting transfers between devices  196 us (40%)
  matrix products  164 us (33%)
  waiting for transfers between devices  70.3 us (14%)
  other arithmetic  47.9 us (10%)
  local copies, waits for them, and re-layouts  10.2 us (2%)
  loops' own time  5.33 us (1%)
    ppermute x56, starting transfers between devices, shift_pair(): return (lax.ppermute(up, axis, forward), lax.ppermute(down, axis, backward))  120 us
    dot_general x28, matrix products, place_split(): lax.dot_general(onehot, weighted.astype(jnp.bfloat16), (((0,), (0,)), (()...  96.1 us
    all_to_all x14, starting transfers between devices, trade_both(): lax.all_to_all(paired, ('slab', 'plane'), split_axis=1, concat_axis=1, ti...  68 us
    all_to_all x14, waiting for transfers between devices, trade_both(): lax.all_to_all(paired, ('slab', 'plane'), split_axis=1, concat_axis=1, ti...  64.9 us
    dot_general x28, matrix products, pick_split(): jnp.dot(onehot.astype(jnp.bfloat16), stacked, preferred_element_type=jnp....  63.1 us
    reduce_sum x28, other arithmetic, membrane(): return (renewed, jnp.sum(driving * renewed, axis=0))  33.5 us
  transfers between devices with their start and end apart: 71, of which 15 were waited for; matrix products, arithmetic and copies ran while one was open for 43% of the time, Pallas kernels for 0%

commit v1 on v0

--- a/solution.py
+++ b/solution.py
@@ -6,6 +6,18 @@
 STEPS = 14
 time_step = 0.1
 gate_slope = 2.0
+
+
+def move_results_now(x_part):
+    return jnp.concatenate(
+        lax.all_to_all(
+            jnp.stack(jnp.split(x_part, lax.axis_size(("slab", "plane")), 1)),
+            ("slab", "plane"),
+            0,
+            0,
+        ),
+        1,
+    )
 
 
 def shift_pair(up, down, axis):
@@ -109,7 +121,7 @@
 
 
 def trade_both(paired):
-    return lax.all_to_all(paired, ("slab", "plane"), split_axis=1, concat_axis=1, tiled=True)
+    return move_results_now(paired)
 
 
 def body(

time: 496 us -> 749 us (1.51)
  local copies, waits for them, and re-layouts: 10.2 us -> 272 us
  other arithmetic: 47.9 us -> 38.2 us
    while x84 -> x532, local copies, waits for them, and re-layouts: 0.41 us -> 254 us
    another operation x42 -> x28, other arithmetic: 9.95 us -> 0.28 us  [the longest x14 9.67 us: advance(): jnp.stack([fibre_at_slot, tissue_at_slot]).reshape(2, devices, capacity)]
    another operation x0 -> x56, local copies, waits for them, and re-layouts: none -> 8.36 us  [the longest x14 7.98 us: move_results_now(): jnp.stack(jnp.split(x_part, lax.axis_size(('slab', 'plane')), 1))]
  transfers between devices with their start and end apart: 71 -> 71, of which waited for: 15 -> 15; matrix products, arithmetic and copies ran while one was open for 43% -> 62% of each run, Pallas kernels for 0% -> 0%
where the time goes in v1:
time: 749 us; the launch traced here: 747 us
  local copies, waits for them, and re-layouts  272 us (36%)
  starting transfers between devices  196 us (26%)
  matrix products  164 us (22%)
  waiting for transfers between devices  70.3 us (9%)
  other arithmetic  38.2 us (5%)
    while x532, local copies, waits for them, and re-layouts  254 us
    ppermute x56, starting transfers between devices, shift_pair(): return (lax.ppermute(up, axis, forward), lax.ppermute(down, axis, backward))  120 us
    dot_general x28, matrix products, place_split(): lax.dot_general(onehot, weighted.astype(jnp.bfloat16), (((0,), (0,)), (()...  96.1 us
    all_to_all x14, starting transfers between devices, move_results_now(): lax.all_to_all(jnp.stack(jnp.split(x_part, lax.axis_size(('slab', 'plane'...  68.1 us
    all_to_all x14, waiting for transfers between devices, move_results_now(): lax.all_to_all(jnp.stack(jnp.split(x_part, lax.axis_size(('slab', 'plane'...  64.9 us
    dot_general x28, matrix products, pick_split(): jnp.dot(onehot.astype(jnp.bfloat16), stacked, preferred_element_type=jnp....  63.2 us
    reduce_sum x28, other arithmetic, membrane(): return (renewed, jnp.sum(driving * renewed, axis=0))  33.5 us
  transfers between devices with their start and end apart: 71, of which 15 were waited for; matrix products, arithmetic and copies ran while one was open for 62% of the time, Pallas kernels for 0%

profile of v1, /device:TPU:0, one launch (start us, length us, event | category | flops | bytes accessed | tf_op | source)
XLA Modules:
  0.0 746.9 jit_solution(17975531711647793903)
XLA Ops:
  5.3 7.3 all-to-all-start.1
  14.7 5.3 all-to-all-done.1
  20.5 725.8 %while.20 = (s32[]{:T(128)}, f32[4,16,128]{2,1,0:T(8,128)S(1)}, f32[40,4,16,128]{3,2,1,0:T(8,128)S(1)}, f32[16,512]{1,0:T(8,128)S(1)}, f32[40,16,512]{2,1,0:T(8,...) while((s32[]{:T(128)}, f32[4,16,128]{2,1,0:T(8,128)S(1)}, ...), condition=%wide.region_8.9_spmd.clone, body=%wide.region_3.8_spmd.clone.sunk | while | flops 1107426560 | bytes 8597641 | solution.py:235
  52.9 4.9 all-to-all-start
  60.6 4.6 all-to-all-done
  104.8 4.9 all-to-all-start
  156.6 4.9 all-to-all-start
  164.2 4.6 all-to-all-done
  208.4 4.9 all-to-all-start
  260.3 4.9 all-to-all-start
  267.9 4.6 all-to-all-done
  312.1 4.9 all-to-all-start
  319.7 4.6 all-to-all-done
  363.9 4.9 all-to-all-start
  371.5 4.6 all-to-all-done
  415.7 4.9 all-to-all-start
  423.4 4.6 all-to-all-done
  467.6 4.9 all-to-all-start
  519.4 4.9 all-to-all-start
  527.0 4.6 all-to-all-done
  571.2 4.9 all-to-all-start
  623.0 4.9 all-to-all-start
  674.9 4.9 all-to-all-start
  726.7 4.9 all-to-all-start
  (1324 shorter events, 626.7 us)
Async XLA Ops:
  20.7 51.6 %collective-permute-start = (f32[1,16,128]{2,1,0:T(8,128)S(1)}, f32[1,16,128]{2,1,0:T(8,128)S(1)}, u32[]{:S(2)}, u32[]{:S(2)}) collective-permute-start(f32[1,16,128]{2,1,0:T(8,128)S(1)} %get-tuple-element.600), channel_id=1, source_target_pairs={{4,0},{8,4},{12,8},{16,12},{20,16},{24,20},{28,24},{5,1},{9,5},{13... | collective-permute-start | bytes 24584 | tf_op jit(solution)/shard_map/while/body/eval_jaxpr/ppermute | solution.py:27
  72.5 51.6 %collective-permute-start = (f32[1,16,128]{2,1,0:T(8,128)S(1)}, f32[1,16,128]{2,1,0:T(8,128)S(1)}, u32[]{:S(2)}, u32[]{:S(2)}) collective-permute-start(f32[1,16,128]{2,1,0:T(8,128)S(1)} %get-tuple-element.600), channel_id=1, source_target_pairs={{4,0},{8,4},{12,8},{16,12},{20,16},{24,20},{28,24},{5,1},{9,5},{13... | collective-permute-start | bytes 24584 | tf_op jit(solution)/shard_map/while/body/eval_jaxpr/ppermute | solution.py:27
  73.8 50.4 %collective-permute-start.1 = (f32[1,16,128]{2,1,0:T(8,128)S(1)}, f32[1,16,128]{2,1,0:T(8,128)S(1)}, u32[]{:S(2)}, u32[]{:S(2)}) collective-permute-start(f32[1,16,128]{2,1,0:T(8,128)S(1)} %get-tuple-element.603), channel_id=1, source_target_pairs={{0,4},{4,8},{8,12},{12,16},{16,20},{20,24},{24,28},{1,5},{5,9},{9,... | collective-permute-start | bytes 24584 | tf_op jit(solution)/shard_map/while/body/eval_jaxpr/ppermute | solution.py:27
  124.4 51.6 %collective-permute-start = (f32[1,16,128]{2,1,0:T(8,128)S(1)}, f32[1,16,128]{2,1,0:T(8,128)S(1)}, u32[]{:S(2)}, u32[]{:S(2)}) collective-permute-start(f32[1,16,128]{2,1,0:T(8,128)S(1)} %get-tuple-element.600), channel_id=1, source_target_pairs={{4,0},{8,4},{12,8},{16,12},{20,16},{24,20},{28,24},{5,1},{9,5},{13... | collective-permute-start | bytes 24584 | tf_op jit(solution)/shard_map/while/body/eval_jaxpr/ppermute | solution.py:27
  125.7 50.4 %collective-permute-start.1 = (f32[1,16,128]{2,1,0:T(8,128)S(1)}, f32[1,16,128]{2,1,0:T(8,128)S(1)}, u32[]{:S(2)}, u32[]{:S(2)}) collective-permute-start(f32[1,16,128]{2,1,0:T(8,128)S(1)} %get-tuple-element.603), channel_id=1, source_target_pairs={{0,4},{4,8},{8,12},{12,16},{16,20},{20,24},{24,28},{1,5},{5,9},{9,... | collective-permute-start | bytes 24584 | tf_op jit(solution)/shard_map/while/body/eval_jaxpr/ppermute | solution.py:27
  176.2 51.6 %collective-permute-start = (f32[1,16,128]{2,1,0:T(8,128)S(1)}, f32[1,16,128]{2,1,0:T(8,128)S(1)}, u32[]{:S(2)}, u32[]{:S(2)}) collective-permute-start(f32[1,16,128]{2,1,0:T(8,128)S(1)} %get-tuple-element.600), channel_id=1, source_target_pairs={{4,0},{8,4},{12,8},{16,12},{20,16},{24,20},{28,24},{5,1},{9,5},{13... | collective-permute-start | bytes 24584 | tf_op jit(solution)/shard_map/while/body/eval_jaxpr/ppermute | solution.py:27
  177.5 50.4 %collective-permute-start.1 = (f32[1,16,128]{2,1,0:T(8,128)S(1)}, f32[1,16,128]{2,1,0:T(8,128)S(1)}, u32[]{:S(2)}, u32[]{:S(2)}) collective-permute-start(f32[1,16,128]{2,1,0:T(8,128)S(1)} %get-tuple-element.603), channel_id=1, source_target_pairs={{0,4},{4,8},{8,12},{12,16},{16,20},{20,24},{24,28},{1,5},{5,9},{9,... | collective-permute-start | bytes 24584 | tf_op jit(solution)/shard_map/while/body/eval_jaxpr/ppermute | solution.py:27
  228.0 51.6 %collective-permute-start = (f32[1,16,128]{2,1,0:T(8,128)S(1)}, f32[1,16,128]{2,1,0:T(8,128)S(1)}, u32[]{:S(2)}, u32[]{:S(2)}) collective-permute-start(f32[1,16,128]{2,1,0:T(8,128)S(1)} %get-tuple-element.600), channel_id=1, source_target_pairs={{4,0},{8,4},{12,8},{16,12},{20,16},{24,20},{28,24},{5,1},{9,5},{13... | collective-permute-start | bytes 24584 | tf_op jit(solution)/shard_map/while/body/eval_jaxpr/ppermute | solution.py:27
  229.3 50.4 %collective-permute-start.1 = (f32[1,16,128]{2,1,0:T(8,128)S(1)}, f32[1,16,128]{2,1,0:T(8,128)S(1)}, u32[]{:S(2)}, u32[]{:S(2)}) collective-permute-start(f32[1,16,128]{2,1,0:T(8,128)S(1)} %get-tuple-element.603), channel_id=1, source_target_pairs={{0,4},{4,8},{8,12},{12,16},{16,20},{20,24},{24,28},{1,5},{5,9},{9,... | collective-permute-start | bytes 24584 | tf_op jit(solution)/shard_map/while/body/eval_jaxpr/ppermute | solution.py:27
  279.8 51.6 %collective-permute-start = (f32[1,16,128]{2,1,0:T(8,128)S(1)}, f32[1,16,128]{2,1,0:T(8,128)S(1)}, u32[]{:S(2)}, u32[]{:S(2)}) collective-permute-start(f32[1,16,128]{2,1,0:T(8,128)S(1)} %get-tuple-element.600), channel_id=1, source_target_pairs={{4,0},{8,4},{12,8},{16,12},{20,16},{24,20},{28,24},{5,1},{9,5},{13... | collective-permute-start | bytes 24584 | tf_op jit(solution)/shard_map/while/body/eval_jaxpr/ppermute | solution.py:27
  281.1 50.4 %collective-permute-start.1 = (f32[1,16,128]{2,1,0:T(8,128)S(1)}, f32[1,16,128]{2,1,0:T(8,128)S(1)}, u32[]{:S(2)}, u32[]{:S(2)}) collective-permute-start(f32[1,16,128]{2,1,0:T(8,128)S(1)} %get-tuple-element.603), channel_id=1, source_target_pairs={{0,4},{4,8},{8,12},{12,16},{16,20},{20,24},{24,28},{1,5},{5,9},{9,... | collective-permute-start | bytes 24584 | tf_op jit(solution)/shard_map/while/body/eval_jaxpr/ppermute | solution.py:27
  331.7 51.6 %collective-permute-start = (f32[1,16,128]{2,1,0:T(8,128)S(1)}, f32[1,16,128]{2,1,0:T(8,128)S(1)}, u32[]{:S(2)}, u32[]{:S(2)}) collective-permute-start(f32[1,16,128]{2,1,0:T(8,128)S(1)} %get-tuple-element.600), channel_id=1, source_target_pairs={{4,0},{8,4},{12,8},{16,12},{20,16},{24,20},{28,24},{5,1},{9,5},{13... | collective-permute-start | bytes 24584 | tf_op jit(solution)/shard_map/while/body/eval_jaxpr/ppermute | solution.py:27
  333.0 50.4 %collective-permute-start.1 = (f32[1,16,128]{2,1,0:T(8,128)S(1)}, f32[1,16,128]{2,1,0:T(8,128)S(1)}, u32[]{:S(2)}, u32[]{:S(2)}) collective-permute-start(f32[1,16,128]{2,1,0:T(8,128)S(1)} %get-tuple-element.603), channel_id=1, source_target_pairs={{0,4},{4,8},{8,12},{12,16},{16,20},{20,24},{24,28},{1,5},{5,9},{9,... | collective-permute-start | bytes 24584 | tf_op jit(solution)/shard_map/while/body/eval_jaxpr/ppermute | solution.py:27
  383.5 51.6 %collective-permute-start = (f32[1,16,128]{2,1,0:T(8,128)S(1)}, f32[1,16,128]{2,1,0:T(8,128)S(1)}, u32[]{:S(2)}, u32[]{:S(2)}) collective-permute-start(f32[1,16,128]{2,1,0:T(8,128)S(1)} %get-tuple-element.600), channel_id=1, source_target_pairs={{4,0},{8,4},{12,8},{16,12},{20,16},{24,20},{28,24},{5,1},{9,5},{13... | collective-permute-start | bytes 24584 | tf_op jit(solution)/shard_map/while/body/eval_jaxpr/ppermute | solution.py:27
  384.8 50.4 %collective-permute-start.1 = (f32[1,16,128]{2,1,0:T(8,128)S(1)}, f32[1,16,128]{2,1,0:T(8,128)S(1)}, u32[]{:S(2)}, u32[]{:S(2)}) collective-permute-start(f32[1,16,128]{2,1,0:T(8,128)S(1)} %get-tuple-element.603), channel_id=1, source_target_pairs={{0,4},{4,8},{8,12},{12,16},{16,20},{20,24},{24,28},{1,5},{5,9},{9,... | collective-permute-start | bytes 24584 | tf_op jit(solution)/shard_map/while/body/eval_jaxpr/ppermute | solution.py:27
  435.3 51.6 %collective-permute-start = (f32[1,16,128]{2,1,0:T(8,128)S(1)}, f32[1,16,128]{2,1,0:T(8,128)S(1)}, u32[]{:S(2)}, u32[]{:S(2)}) collective-permute-start(f32[1,16,128]{2,1,0:T(8,128)S(1)} %get-tuple-element.600), channel_id=1, source_target_pairs={{4,0},{8,4},{12,8},{16,12},{20,16},{24,20},{28,24},{5,1},{9,5},{13... | collective-permute-start | bytes 24584 | tf_op jit(solution)/shard_map/while/body/eval_jaxpr/ppermute | solution.py:27
  436.6 50.4 %collective-permute-start.1 = (f32[1,16,128]{2,1,0:T(8,128)S(1)}, f32[1,16,128]{2,1,0:T(8,128)S(1)}, u32[]{:S(2)}, u32[]{:S(2)}) collective-permute-start(f32[1,16,128]{2,1,0:T(8,128)S(1)} %get-tuple-element.603), channel_id=1, source_target_pairs={{0,4},{4,8},{8,12},{12,16},{16,20},{20,24},{24,28},{1,5},{5,9},{9,... | collective-permute-start | bytes 24584 | tf_op jit(solution)/shard_map/while/body/eval_jaxpr/ppermute | solution.py:27
  487.1 51.6 %collective-permute-start = (f32[1,16,128]{2,1,0:T(8,128)S(1)}, f32[1,16,128]{2,1,0:T(8,128)S(1)}, u32[]{:S(2)}, u32[]{:S(2)}) collective-permute-start(f32[1,16,128]{2,1,0:T(8,128)S(1)} %get-tuple-element.600), channel_id=1, source_target_pairs={{4,0},{8,4},{12,8},{16,12},{20,16},{24,20},{28,24},{5,1},{9,5},{13... | collective-permute-start | bytes 24584 | tf_op jit(solution)/shard_map/while/body/eval_jaxpr/ppermute | solution.py:27
  488.4 50.4 %collective-permute-start.1 = (f32[1,16,128]{2,1,0:T(8,128)S(1)}, f32[1,16,128]{2,1,0:T(8,128)S(1)}, u32[]{:S(2)}, u32[]{:S(2)}) collective-permute-start(f32[1,16,128]{2,1,0:T(8,128)S(1)} %get-tuple-element.603), channel_id=1, source_target_pairs={{0,4},{4,8},{8,12},{12,16},{16,20},{20,24},{24,28},{1,5},{5,9},{9,... | collective-permute-start | bytes 24584 | tf_op jit(solution)/shard_map/while/body/eval_jaxpr/ppermute | solution.py:27
  539.0 51.6 %collective-permute-start = (f32[1,16,128]{2,1,0:T(8,128)S(1)}, f32[1,16,128]{2,1,0:T(8,128)S(1)}, u32[]{:S(2)}, u32[]{:S(2)}) collective-permute-start(f32[1,16,128]{2,1,0:T(8,128)S(1)} %get-tuple-element.600), channel_id=1, source_target_pairs={{4,0},{8,4},{12,8},{16,12},{20,16},{24,20},{28,24},{5,1},{9,5},{13... | collective-permute-start | bytes 24584 | tf_op jit(solution)/shard_map/while/body/eval_jaxpr/ppermute | solution.py:27
  540.3 50.4 %collective-permute-start.1 = (f32[1,16,128]{2,1,0:T(8,128)S(1)}, f32[1,16,128]{2,1,0:T(8,128)S(1)}, u32[]{:S(2)}, u32[]{:S(2)}) collective-permute-start(f32[1,16,128]{2,1,0:T(8,128)S(1)} %get-tuple-element.603), channel_id=1, source_target_pairs={{0,4},{4,8},{8,12},{12,16},{16,20},{20,24},{24,28},{1,5},{5,9},{9,... | collective-permute-start | bytes 24584 | tf_op jit(solution)/shard_map/while/body/eval_jaxpr/ppermute | solution.py:27
  590.8 51.6 %collective-permute-start = (f32[1,16,128]{2,1,0:T(8,128)S(1)}, f32[1,16,128]{2,1,0:T(8,128)S(1)}, u32[]{:S(2)}, u32[]{:S(2)}) collective-permute-start(f32[1,16,128]{2,1,0:T(8,128)S(1)} %get-tuple-element.600), channel_id=1, source_target_pairs={{4,0},{8,4},{12,8},{16,12},{20,16},{24,20},{28,24},{5,1},{9,5},{13... | collective-permute-start | bytes 24584 | tf_op jit(solution)/shard_map/while/body/eval_jaxpr/ppermute | solution.py:27
  642.6 51.6 %collective-permute-start = (f32[1,16,128]{2,1,0:T(8,128)S(1)}, f32[1,16,128]{2,1,0:T(8,128)S(1)}, u32[]{:S(2)}, u32[]{:S(2)}) collective-permute-start(f32[1,16,128]{2,1,0:T(8,128)S(1)} %get-tuple-element.600), channel_id=1, source_target_pairs={{4,0},{8,4},{12,8},{16,12},{20,16},{24,20},{28,24},{5,1},{9,5},{13... | collective-permute-start | bytes 24584 | tf_op jit(solution)/shard_map/while/body/eval_jaxpr/ppermute | solution.py:27
  694.5 51.6 %collective-permute-start = (f32[1,16,128]{2,1,0:T(8,128)S(1)}, f32[1,16,128]{2,1,0:T(8,128)S(1)}, u32[]{:S(2)}, u32[]{:S(2)}) collective-permute-start(f32[1,16,128]{2,1,0:T(8,128)S(1)} %get-tuple-element.600), channel_id=1, source_target_pairs={{4,0},{8,4},{12,8},{16,12},{20,16},{24,20},{28,24},{5,1},{9,5},{13... | collective-permute-start | bytes 24584 | tf_op jit(solution)/shard_map/while/body/eval_jaxpr/ppermute | solution.py:27
  (121 other events, 1738.0 us)
